TPU v7x, 256 devices: a whole 4x4x8 slice. The times are simulated.
256 devices in a mesh: lat: 128 (over x, z, y), lev: 2 (over core).
Axes of the slice: x: 4, y: 4, z: 8, core: 2. Of those that a mesh axis runs over, the one named last changes fastest.
Arguments:
- fields: float32 [1280, 3, 16, 2560], P('lat', None, 'lev'), may hold values from 0.1 to 5
- lat_fraction: float32 [1280], P('lat'), may hold values from 0 to 1
- lon_fraction: float32 [1280], P('lat'), may hold values from 0 to 1
- lon_shift: int32 [1280], P('lat'), may hold values from 0 to 2559
- departure_row: int32 [1280], P('lat'), may hold values from 1 to 1277, as said below
- extents: int32 [128, 2], P('lat'), may hold values from 1 to 4
Outputs:
- advected: float32 [1280, 3, 16, 2560], P('lat', None, 'lev')
Inputs may be any that keep to these rules, and one draw needn't show every extreme that they name: departure_row[r] lies within 39 rows of r.
All inputs are finite; a program needn't handle non-finite values.
Results may differ from a plain program's by a relative error of at most 0.0003.
Values sent between devices are 32-bit elements; how exact they have to be, the bound alone decides.
A program may use at most 128 MiB of HBM per device.

v0:
```python
import functools
import math

import jax
import jax.numpy as jnp
import numpy as np
from jax import lax
from jax.experimental import pallas as pl
from jax.experimental.pallas import tpu as pltpu
from jax.sharding import PartitionSpec as P

REACH = 4
LANES = 128
DEPTH = 5
MESH = pl.DeviceIdType.MESH

UP = {
    0: [],
    1: [(0, 1), (0, 2), (0, 0)],
    2: [(0, 0), (0, 1), (0, 2), (1, 0)],
    3: [(1, 1), (1, 2), (1, 0), (0, 0)],
}
UP_OVER_ONE = {3: [(2, 0), (2, 1), (2, 2)], 2: [(1, 1), (1, 2)]}
UP_OVER_TWO = {3: [(0, 1), (0, 2)]}


def arrivals(member):
    def both(table):
        up = [(1, m, h) for m, h in table.get(member, [])]
        down = [(-1, 3 - m, h) for m, h in table.get(3 - member, [])]
        return up + down

    one = [(0, member ^ 1, h) for h in range(3)] + [(0, member ^ 3, 0)] + both(UP_OVER_ONE)
    two = [(0, member ^ 2, h) for h in range(3)] + [(0, member ^ 3, h) for h in (1, 2)] + both(UP_OVER_TWO)
    up = [(1, member, h) for h in range(3)] + [(1, m, h) for m, h in UP[member]]
    down = [(-1, member, h) for h in range(3)] + [(-1, 3 - m, h) for m, h in UP[3 - member]]
    return {"one": one, "two": two, "up": up, "down": down}


LINKS = ("one", "two", "up", "down")


def cubic(t):
    sixth = 1.0 / 6.0
    return (
        -t * (t - 1.0) * (t - 2.0) * sixth,
        (t + 1.0) * (t - 1.0) * (t - 2.0) * 0.5,
        -(t + 1.0) * t * (t - 2.0) * 0.5,
        (t + 1.0) * t * (t - 1.0) * sixth,
    )


def departure_of(row, first_row, rows, total_rows, departure_ref, extents_ref):
    low = first_row - extents_ref[0, 0] * rows + 1
    high = first_row + rows - 3 + extents_ref[0, 1] * rows
    inside = jnp.minimum(jnp.maximum(departure_ref[row], low), high)
    return jnp.minimum(jnp.maximum(inside, 1), total_rows - 3)


def exchange_kernel(bands, levs, lat_t_ref, lon_t_ref, departure_ref, extents_ref, area_ref, fields_ref,
                    halo_ref, table_ref, held, mine, met, sent, gathered, send_sem, recv_sem, local_sem,
                    table_send_sem, table_recv_sem):
    band, lev = lax.axis_index("lat"), lax.axis_index("lev")
    group, position = band // 4, lax.rem(band, 4)
    groups = bands // 4
    has_up = group < groups - 1
    has_down = group > 0
    rows, field_count = fields_ref.shape[:2]
    first_row, total_rows = band * rows, bands * rows
    step_one = 1 - 2 * lax.rem(position, 2)
    step_two = 2 - 4 * (position // 2)
    across = [{"lev": 1 - lev}, {"lat": band + step_one}, {"lat": band + step_two}]
    others = [{"lat": lax.rem(band + 4 * j, bands)} for j in range(1, groups)]

    barrier = pltpu.get_barrier_semaphore()
    for peer in across + others:
        pl.semaphore_signal(barrier, inc=1, device_id=peer, device_id_type=MESH)
    pl.semaphore_wait(barrier, len(across) + len(others))

    def cut(part):
        first = field_count * part // 3
        return pl.ds(first, field_count * (part + 1) // 3 - first)

    def halo_part(distance, part):
        slot = distance + 4 if distance < 0 else distance + 3
        return halo_ref.at[pl.ds(slot * rows, rows), cut(part)]

    def when(offset, body):
        if offset == 0:
            body()
        else:
            pl.when(has_up if offset == 1 else has_down)(body)

    came_over = [
        {item: (link, k) for link, items in arrivals(member).items() for k, item in enumerate(items)}
        for member in range(4)
    ]
    waited = [set() for _ in range(4)]

    def wait_for(member, item):
        if item in waited[member]:
            return
        waited[member].add(item)
        offset, m, h = item
        link, k = came_over[member][item]
        place = halo_part(4 * offset + m - member, h)
        when(
            offset,
            lambda: pltpu.make_async_remote_copy(
                src_ref=place, dst_ref=place,
                send_sem=send_sem.at[LINKS.index(link), k],
                recv_sem=recv_sem.at[LINKS.index(link), k],
                device_id={"lat": band}, device_id_type=MESH,
            ).wait_recv(),
        )

    def targets(member):
        return [
            ("up", member, -4, -1),
            ("down", member, 4, 1),
            ("one", member ^ 1, (member ^ 1) - member, 0),
            ("two", member ^ 2, (member ^ 2) - member, 0),
        ]

    def sends(member, k):
        for link, target, step, group_step in targets(member):
            items = arrivals(target)[link]
            if k < len(items):
                offset, m, h = items[k]
                here = offset + group_step
                own = here == 0 and m == member
                copy = pltpu.make_async_remote_copy(
                    src_ref=fields_ref.at[:, cut(h)] if own else halo_part(4 * here + m - member, h),
                    dst_ref=halo_part(4 * offset + m - target, h),
                    send_sem=send_sem.at[LINKS.index(link), k],
                    recv_sem=recv_sem.at[LINKS.index(link), k],
                    device_id={"lat": band + step}, device_id_type=MESH,
                )
                yield (None if own else (here, m, h)), (group_step if group_step else here), copy

    def on_each(body):
        for member in range(4):
            pl.when(position == member)(functools.partial(body, member))

    def send_pieces(*steps):
        def body(member):
            for k in steps:
                for item, condition, copy in sends(member, k):
                    if item is not None:
                        wait_for(member, item)
                    when(condition, copy.start)

        on_each(body)

    def table_copy(n, source, target, peer):
        return pltpu.make_async_remote_copy(
            src_ref=source, dst_ref=target, send_sem=table_send_sem.at[n], recv_sem=table_recv_sem.at[n],
            device_id=peer, device_id_type=MESH,
        )

    load = pltpu.make_async_copy(fields_ref, held, local_sem)
    load.start()
    send_pieces(0)

    lane = lax.broadcasted_iota(jnp.int32, (1, table_ref.shape[1]), 1)
    taken = jnp.zeros(lane.shape, jnp.float32)
    for row in range(rows):
        departure = departure_of(row, first_row, rows, total_rows, departure_ref, extents_ref)
        lon_w = cubic(lon_t_ref[row])
        share = area_ref[first_row + row] * (lon_w[0] + lon_w[1] + lon_w[2] + lon_w[3]) * (1.0 / levs)
        for a, weight in enumerate(cubic(lat_t_ref[row])):
            taken = taken + jnp.where(lane == departure - 1 + a, share * weight, 0.0)
    load.wait()
    sums = [jnp.zeros(lane.shape, jnp.float32) for _ in range(field_count)]
    for row in range(rows):
        for f in range(field_count):
            total = jnp.sum(jnp.sum(held[row, f], axis=0, keepdims=True), axis=1, keepdims=True)
            sums[f] = sums[f] + jnp.where(lane == first_row + row, total, 0.0)
    mine[...] = jnp.zeros_like(mine)
    for f in range(field_count):
        mine[f:f + 1, :] = sums[f]
    mine[field_count:field_count + 1, :] = taken

    def table_step(n):
        return table_copy(n, mine if n == 0 else sent.at[n - 1], met.at[n], across[n])

    def table_add(n):
        table_step(n).wait_recv()
        sent[n] = (mine[...] if n == 0 else sent[n - 1]) + met[n]

    table_step(0).start()
    table_add(0)
    table_step(1).start()
    send_pieces(1, 2)
    table_add(1)
    table_step(2).start()
    send_pieces(3, 4)
    table_add(2)
    last = [table_copy(3 + j, sent.at[2], gathered.at[j], peer) for j, peer in enumerate(others)]
    for copy in last:
        copy.start()
    send_pieces(5, 6)
    for copy in last:
        copy.wait_recv()
    result = sent[2]
    for j in range(len(others)):
        result = result + gathered[j]
    table_ref[...] = result

    def finish(member):
        for k in range(7):
            for link in LINKS:
                items = arrivals(member)[link]
                if k < len(items):
                    wait_for(member, items[k])
        for k in range(7):
            for _, condition, copy in sends(member, k):
                when(condition, copy.wait_send)

    on_each(finish)
    for n in range(3):
        table_step(n).wait_send()
    for copy in last:
        copy.wait_send()


def exchange(lat_t, lon_t, departure_row, extents, area, fields):
    bands, levs = lax.axis_size("lat"), lax.axis_size("lev")
    rows, field_count = fields.shape[:2]
    table = ((field_count + 8) // 8 * 8, -(-bands * rows // LANES) * LANES)
    others = bands // 4 - 1
    return pl.pallas_call(
        functools.partial(exchange_kernel, bands, levs),
        out_shape=(
            jax.ShapeDtypeStruct((2 * REACH * rows,) + fields.shape[1:], fields.dtype),
            jax.ShapeDtypeStruct(table, jnp.float32),
        ),
        in_specs=[pl.BlockSpec(memory_space=pltpu.SMEM)] * 5 + [pl.BlockSpec(memory_space=pl.ANY)],
        out_specs=(pl.BlockSpec(memory_space=pl.ANY), pl.BlockSpec(memory_space=pltpu.VMEM)),
        scratch_shapes=[
            pltpu.VMEM(fields.shape, jnp.float32),
            pltpu.VMEM(table, jnp.float32),
            pltpu.VMEM((3,) + table, jnp.float32),
            pltpu.VMEM((3,) + table, jnp.float32),
            pltpu.VMEM((max(others, 1),) + table, jnp.float32),
            pltpu.SemaphoreType.DMA((4, 7)),
            pltpu.SemaphoreType.DMA((4, 7)),
            pltpu.SemaphoreType.DMA,
            pltpu.SemaphoreType.DMA((3 + others,)),
            pltpu.SemaphoreType.DMA((3 + others,)),
        ],
        compiler_params=pltpu.CompilerParams(collective_id=0, has_side_effects=True),
        name="exchange",
    )(lat_t, lon_t, departure_row, extents, area, fields)


def row_kernel(bands, lat_t_ref, lon_t_ref, shift_ref, departure_ref, extents_ref, table_ref, area_ref, fields_ref,
               halo_ref, out_ref, held, doubled, ratio, sem):
    row = pl.program_id(0)
    row_count = pl.num_programs(0)
    rows, field_count, _, lon_count = fields_ref.shape
    tiles = lon_count // LANES
    depth = held.shape[0]
    first_row = lax.axis_index("lat") * rows

    def fetch(index):
        slot = lax.rem(index, depth)
        departure = departure_of(index, first_row, rows, bands * rows, departure_ref, extents_ref)
        start = departure - 1 - (first_row - REACH * rows)
        low, high = REACH * rows, (REACH + 1) * rows
        outside = jnp.logical_or(start + 4 <= low, start >= high)

        @pl.when(outside)
        def _():
            away = jnp.where(start < low, start, start - rows)
            pltpu.make_async_copy(halo_ref.at[pl.ds(away, 4)], held.at[slot], sem.at[slot]).start()

        @pl.when(jnp.logical_not(outside))
        def _():
            for a in range(4):
                place = start + a
                own = jnp.logical_and(place >= low, place < high)
                target = held.at[slot, a]

                @pl.when(own)
                def _():
                    pltpu.make_async_copy(fields_ref.at[place - low], target, sem.at[slot]).start()

                @pl.when(jnp.logical_not(own))
                def _():
                    away = jnp.where(place < low, place, place - rows)
                    pltpu.make_async_copy(halo_ref.at[away], target, sem.at[slot]).start()

    @pl.when(row == 0)
    def _():
        for index in range(min(depth - 1, rows)):
            fetch(index)
        weight = table_ref[field_count:field_count + 1, :]
        for f in range(field_count):
            total = table_ref[f:f + 1, :]
            before = jnp.sum(total * area_ref[...], axis=1, keepdims=True)
            after = jnp.sum(total * weight, axis=1, keepdims=True)
            ratio[f] = jnp.broadcast_to(before / after, ratio.shape[1:])

    @pl.when(row + depth - 1 < row_count)
    def _():
        fetch(row + depth - 1)

    slot = lax.rem(row, depth)
    pltpu.make_async_copy(halo_ref.at[pl.ds(0, 4)], held.at[slot], sem.at[slot]).wait()
    lat_w, lon_w = cubic(lat_t_ref[row]), cubic(lon_t_ref[row])
    lane = lax.broadcasted_iota(jnp.int32, (out_ref.shape[2], LANES), 1)
    first = lax.rem(shift_ref[row] - 1 + lon_count, lon_count)
    whole, rest = first // LANES, lax.rem(first, LANES)
    turn = lax.rem(LANES - rest, LANES)
    keep = lane < LANES - rest

    def ahead(pieces, step):
        turned = [pltpu.roll(piece, LANES - step, 1) for piece in pieces]
        return [jnp.where(lane < LANES - step, turned[t], turned[(t + 1) % tiles]) for t in range(tiles)]

    for f in range(field_count):
        lon = [weight * ratio[f] for weight in lon_w]
        column = []
        for t in range(tiles):
            at = pl.ds(t * LANES, LANES)
            total = lat_w[0] * held[slot, 0, f, :, at]
            for a in range(1, 4):
                total = total + lat_w[a] * held[slot, a, f, :, at]
            column.append(total)
        after = ahead(column, 1)
        later = ahead([lon[2] * column[t] + lon[3] * after[t] for t in range(tiles)], 2)
        for t in range(tiles):
            mixed = lon[0] * column[t] + lon[1] * after[t] + later[t]
            doubled[f, :, t * LANES:(t + 1) * LANES] = mixed
            doubled[f, :, lon_count + t * LANES:lon_count + (t + 1) * LANES] = mixed
        turned = []
        for t in range(tiles + 1):
            at = pl.multiple_of((whole + t) * LANES, LANES)
            turned.append(pltpu.roll(doubled[f, :, pl.ds(at, LANES)], turn, 1))
        for t in range(tiles):
            out_ref[0, f, :, t * LANES:(t + 1) * LANES] = jnp.where(keep, turned[t], turned[t + 1])


def rows_of(bands, lat_t, lon_t, shift, departure_row, extents, table, area, fields, halo):
    rows, field_count, levels, lon_count = fields.shape
    smem = pl.BlockSpec(memory_space=pltpu.SMEM)
    return pl.pallas_call(
        functools.partial(row_kernel, bands),
        grid=(rows,),
        out_shape=jax.ShapeDtypeStruct(fields.shape, fields.dtype),
        in_specs=[smem] * 5 + [pl.BlockSpec(memory_space=pltpu.VMEM)] * 2 + [pl.BlockSpec(memory_space=pl.ANY)] * 2,
        out_specs=pl.BlockSpec((1, field_count, levels, lon_count), lambda r: (r, 0, 0, 0)),
        scratch_shapes=[
            pltpu.VMEM((DEPTH, 4, field_count, levels, lon_count), jnp.float32),
            pltpu.VMEM((field_count, levels, 2 * lon_count), jnp.float32),
            pltpu.VMEM((field_count, levels, LANES), jnp.float32),
            pltpu.SemaphoreType.DMA((DEPTH,)),
        ],
        compiler_params=pltpu.CompilerParams(dimension_semantics=("arbitrary",)),
        name="rows",
    )(lat_t, lon_t, shift, departure_row, extents, table, area, fields, halo)


def per_device(fields, lat_fraction, lon_fraction, lon_shift, departure_row, extents):
    bands = lax.axis_size("lat")
    total_rows = bands * fields.shape[0]
    row_ids = np.arange(-(-total_rows // LANES) * LANES)
    area = np.where(row_ids < total_rows, np.cos(math.pi * (row_ids + 0.5) / total_rows - math.pi / 2.0), 0.0)
    area = jnp.asarray(area, jnp.float32)
    halo, table = exchange(lat_fraction, lon_fraction, departure_row, extents, area, fields)
    return rows_of(
        bands, lat_fraction, lon_fraction, lon_shift, departure_row, extents, table, area[None, :], fields, halo
    )


def solution(mesh):
    return jax.shard_map(
        per_device,
        mesh=mesh,
        in_specs=(
            P("lat", None, "lev", None),
            P("lat"),
            P("lat"),
            P("lat"),
            P("lat"),
            P("lat", None),
        ),
        out_specs=P("lat", None, "lev", None),
        check_vma=False,
    )
```

profile of v0, /device:TPU:32, one launch (start us, length us, event | category | flops | bytes accessed | tf_op | source)
XLA Modules:
  0.0 271.0 jit_solution(4080694119024886351)
XLA Ops:
  0.0 263.2 %exchange.1 = (f32[80,3,8,2560]{3,2,1,0:T(8,128)}, f32[8,1280]{1,0:T(8,128)}) custom-call(f32[10]{0:T(128)} %lat_t_ref.3, f32[10]{0:T(128)} %lon_t_ref.3, s32[10]{0:T(128)} %departure_ref.3, s32[1,2]{1,0:T(1,128)} %extents_ref.3, f32[1280]{0:T(1024)} %constant.2.clone.area_ref, f32[10,3,8,2560]{3,2,1,0:T(8,128)} %fields_ref.3), custom_call_target="tpu_custom_call" | custom-call | tf_op jit(solution)/shard_map/exchange/pallas_call | solution.py:232
  263.2 7.8 %rows.1 = f32[10,3,8,2560]{3,2,1,0:T(8,128)} custom-call(f32[10]{0:T(128)} %lat_t_ref.3, f32[10]{0:T(128)} %lon_t_ref.3, s32[10]{0:T(128)} %shift_ref.1, s32[10]{0:T(128)} %departure_ref.3, s32[1,2]{1,0:T(1,128)} %extents_ref.3, f32[8,1280]{1,0:T(8,128)} %get-tuple-element.7.table_ref, f32[1,1280]{1,0:T(1,128)} %constant.9.area_ref, ...), custom_call_target="tpu_custom_call" | custom-call | tf_op jit(solution)/shard_map/rows/pallas_call | solution.py:348
where the time goes:
time: 271 us
  Pallas kernels  271 us (100%)
    pallas_call x1, Pallas kernels, exchange(): pl.pallas_call(functools.partial(exchange_kernel, bands, levs), out_shape...  263 us
    pallas_call x1, Pallas kernels, rows_of(): pl.pallas_call(functools.partial(row_kernel, bands), grid=(rows,), out_sh...  7.81 us

commit v1 on v0

v1 whole, which is shorter than its diff:
```python
import functools
import math

import jax
import jax.numpy as jnp
import numpy as np
from jax import lax
from jax.experimental import pallas as pl
from jax.experimental.pallas import tpu as pltpu
from jax.sharding import PartitionSpec as P

REACH = 4
LANES = 128
RING = 4
DEEP = 8
MESH = pl.DeviceIdType.MESH


def cubic(t):
    sixth = 1.0 / 6.0
    return (
        -t * (t - 1.0) * (t - 2.0) * sixth,
        (t + 1.0) * (t - 1.0) * (t - 2.0) * 0.5,
        -(t + 1.0) * t * (t - 2.0) * 0.5,
        (t + 1.0) * t * (t - 1.0) * sixth,
    )


def departure_of(row, first_row, rows, total_rows, departure_ref, extents_ref):
    low = first_row - extents_ref[0, 0] * rows + 1
    high = first_row + rows - 3 + extents_ref[0, 1] * rows
    inside = jnp.minimum(jnp.maximum(departure_ref[row], low), high)
    return jnp.minimum(jnp.maximum(inside, 1), total_rows - 3)


def exchange_kernel(bands, levs, lat_t_ref, lon_t_ref, departure_ref, extents_ref, area_ref, fields_ref,
                    out_ref, sums_ref, *scratch):
    rows, field_count, _, lon_count = fields_ref.shape
    held = scratch[0]
    window = scratch[1:1 + field_count]
    column = scratch[1 + field_count:1 + 2 * field_count]
    (real_meta, whole_meta, real_smem, whole_smem, part, met_one, met_two, met_three,
     load_sem, own_sem, smem_sem, meta_send, meta_recv, out_send, out_recv, halo_send, halo_recv,
     back_send, back_recv, one_send, one_recv, two_send, two_recv, three_send, three_recv,
     ) = scratch[1 + 2 * field_count:]
    band, lev = lax.axis_index("lat"), lax.axis_index("lev")
    group, member = band // RING, lax.rem(band, RING)
    groups = bands // RING
    crosses = groups // DEEP
    deep, cross = lax.rem(group, DEEP), group // DEEP
    first_row, total_rows = band * rows, bands * rows
    span = RING * rows
    piece = lon_count // RING

    def ring_member(step):
        return lax.rem(member + step, RING)

    def ring_peer(step):
        return group * RING + ring_member(step)

    def inside(distance):
        place = band + distance
        return jnp.logical_and(place >= 0, place < bands)

    near = [d for d in range(-REACH, REACH + 1) if d != 0]
    one_peers = [(dy, dl) for dy in range(RING) for dl in range(levs) if (dy, dl) != (0, 0)]

    def one_peer(dy, dl):
        return {"lat": ring_peer(dy), "lev": lax.rem(lev + dl, levs)}

    def two_peer(dx):
        return {"lat": (lax.rem(cross + dx, crosses) * DEEP + deep) * RING + member}

    def three_peer(dz):
        return {"lat": (cross * DEEP + lax.rem(deep + dz, DEEP)) * RING + member}

    barrier = pltpu.get_barrier_semaphore()

    def greet(peer):
        pl.semaphore_signal(barrier, inc=1, device_id=peer, device_id_type=MESH)

    for d in near:
        pl.when(inside(d))(functools.partial(greet, {"lat": band + d}))
    for dy, dl in one_peers:
        greet(one_peer(dy, dl))
    for dx in range(1, crosses):
        greet(two_peer(dx))
    for dz in range(1, DEEP):
        greet(three_peer(dz))

    load = pltpu.make_async_copy(fields_ref, held, load_sem)
    load.start()
    own_pieces = []
    for f in range(field_count):
        copy = pltpu.make_async_copy(
            fields_ref.at[:, f, :, pl.ds(pl.multiple_of(member * piece, LANES), piece)],
            window[f].at[pl.ds(span + member * rows, rows)],
            own_sem.at[0, f],
        )
        copy.start()
        own_pieces.append(copy)

    lane = lax.broadcasted_iota(jnp.int32, (1, LANES), 1)
    lat_t = jnp.zeros((1, LANES), jnp.float32)
    lon_t = jnp.zeros((1, LANES), jnp.float32)
    area = jnp.zeros((1, LANES), jnp.float32)
    start = jnp.zeros((1, LANES), jnp.int32)
    for row in range(rows):
        here = lane == row
        lat_t = jnp.where(here, lat_t_ref[row], lat_t)
        lon_t = jnp.where(here, lon_t_ref[row], lon_t)
        area = jnp.where(here, area_ref[first_row + row], area)
        departure = departure_of(row, first_row, rows, total_rows, departure_ref, extents_ref)
        start = jnp.where(here, departure - 1, start)
    lon_w = cubic(lon_t)
    for d in near:
        @pl.when(jnp.logical_not(inside(d)))
        def _(d=d):
            real_meta[REACH + d] = jnp.zeros(real_meta.shape[1:], jnp.float32)
            whole_meta[REACH + d] = jnp.zeros(whole_meta.shape[1:], jnp.int32)
    real_meta[REACH] = jnp.concatenate(
        [*cubic(lat_t), area * (lon_w[0] + lon_w[1] + lon_w[2] + lon_w[3]), jnp.zeros((3, LANES), jnp.float32)], axis=0
    )
    whole_meta[REACH] = jnp.broadcast_to(start, whole_meta.shape[1:])

    expected = len(one_peers) + (crosses - 1) + (DEEP - 1)
    for d in near:
        expected = expected + inside(d).astype(jnp.int32)
    pl.semaphore_wait(barrier, expected)

    def meta_copies(d):
        k = near.index(d)
        return [
            pltpu.make_async_remote_copy(
                src_ref=ref.at[REACH], dst_ref=ref.at[REACH - d],
                send_sem=meta_send.at[n, k], recv_sem=meta_recv.at[n, near.index(-d)],
                device_id={"lat": band + d}, device_id_type=MESH,
            )
            for n, ref in enumerate((real_meta, whole_meta))
        ]

    def meta_arrivals(d):
        k = near.index(d)
        return [
            pltpu.make_async_remote_copy(
                src_ref=ref.at[REACH + d], dst_ref=ref.at[REACH + d],
                send_sem=meta_send.at[n, k], recv_sem=meta_recv.at[n, k],
                device_id={"lat": band + d}, device_id_type=MESH,
            )
            for n, ref in enumerate((real_meta, whole_meta))
        ]

    for d in near:
        @pl.when(inside(d))
        def _(d=d):
            for copy in meta_copies(d):
                copy.start()

    def out_copy(f, dy):
        to = ring_member(dy)
        return pltpu.make_async_remote_copy(
            src_ref=fields_ref.at[:, f, :, pl.ds(pl.multiple_of(to * piece, LANES), piece)],
            dst_ref=window[f].at[pl.ds(span + member * rows, rows)],
            send_sem=out_send.at[f, dy - 1], recv_sem=out_recv.at[f, dy - 1],
            device_id={"lat": ring_peer(dy)}, device_id_type=MESH,
        )

    def out_arrival(f, dy):
        place = window[f].at[pl.ds(span + ring_member(RING - dy) * rows, rows)]
        return pltpu.make_async_remote_copy(
            src_ref=place, dst_ref=place, send_sem=out_send.at[f, dy - 1], recv_sem=out_recv.at[f, dy - 1],
            device_id={"lat": ring_peer(RING - dy)}, device_id_type=MESH,
        )

    has_side = (group < groups - 1, group > 0)

    def halo_copy(f, dy, side):
        who = ring_member(RING - dy)
        if dy == 0:
            source = fields_ref.at[:, f, :, pl.ds(pl.multiple_of(member * piece, LANES), piece)]
        else:
            source = window[f].at[pl.ds(span + who * rows, rows)]
        return pltpu.make_async_remote_copy(
            src_ref=source,
            dst_ref=window[f].at[pl.ds((0 if side == 0 else 2 * span) + who * rows, rows)],
            send_sem=halo_send.at[side, f, dy], recv_sem=halo_recv.at[side, f, dy],
            device_id={"lat": band + (RING if side == 0 else -RING)}, device_id_type=MESH,
        )

    def halo_arrival(f, dy, side):
        place = window[f].at[pl.ds((0 if side == 0 else 2 * span) + ring_member(RING - dy) * rows, rows)]
        return pltpu.make_async_remote_copy(
            src_ref=place, dst_ref=place, send_sem=halo_send.at[side, f, dy], recv_sem=halo_recv.at[side, f, dy],
            device_id={"lat": band + (-RING if side == 0 else RING)}, device_id_type=MESH,
        )

    def start_halo(f, dy):
        for side in range(2):
            pl.when(has_side[side])(lambda side=side: halo_copy(f, dy, side).start())

    def back_copy(f, dy):
        return pltpu.make_async_remote_copy(
            src_ref=column[f].at[pl.ds(dy * rows, rows)],
            dst_ref=out_ref.at[:, f, :, pl.ds(pl.multiple_of(member * piece, LANES), piece)],
            send_sem=back_send.at[f, dy - 1], recv_sem=back_recv.at[f, dy - 1],
            device_id={"lat": ring_peer(dy)}, device_id_type=MESH,
        )

    def back_arrival(f, dy):
        place = out_ref.at[:, f, :, pl.ds(pl.multiple_of(ring_member(RING - dy) * piece, LANES), piece)]
        return pltpu.make_async_remote_copy(
            src_ref=place, dst_ref=place, send_sem=back_send.at[f, dy - 1], recv_sem=back_recv.at[f, dy - 1],
            device_id={"lat": ring_peer(RING - dy)}, device_id_type=MESH,
        )

    def back_own(f):
        return pltpu.make_async_copy(
            column[f].at[pl.ds(0, rows)],
            out_ref.at[:, f, :, pl.ds(pl.multiple_of(member * piece, LANES), piece)],
            own_sem.at[1, f],
        )

    def small_copy(source, target, sends, arrivals, k, peer):
        return pltpu.make_async_remote_copy(
            src_ref=source, dst_ref=target.at[k], send_sem=sends.at[k], recv_sem=arrivals.at[k],
            device_id=peer, device_id_type=MESH,
        )

    ones = [small_copy(part.at[0], met_one, one_send, one_recv, k, one_peer(*p)) for k, p in enumerate(one_peers)]
    twos = [small_copy(part.at[1], met_two, two_send, two_recv, dx - 1, two_peer(dx)) for dx in range(1, crosses)]
    threes = [small_copy(part.at[2], met_three, three_send, three_recv, dz - 1, three_peer(dz)) for dz in range(1, DEEP)]

    order = (1, RING - 1, *range(2, RING - 1))
    for dy in order:
        out_copy(0, dy).start()
    start_halo(0, 0)
    start_halo(1, 0)

    for d in near:
        @pl.when(inside(d))
        def _(d=d):
            for copy in meta_arrivals(d):
                copy.wait_recv()
    group_slots = pl.ds(REACH - member, RING)
    to_smem = [
        pltpu.make_async_copy(real_meta.at[group_slots], real_smem, smem_sem.at[0]),
        pltpu.make_async_copy(whole_meta.at[group_slots], whole_smem, smem_sem.at[1]),
    ]
    for copy in to_smem:
        copy.start()
    load.wait()

    def add_row(row, totals):
        taken = jnp.zeros((2 * REACH + 1, LANES), jnp.float32)
        for a in range(4):
            hit = whole_meta[:, 0, :] + a == first_row + row
            taken = taken + jnp.where(hit, real_meta[:, a, :] * real_meta[:, 4, :], 0.0)
        taken = jnp.sum(jnp.sum(taken, axis=0, keepdims=True), axis=1, keepdims=True)
        row_area = area_ref[first_row + row]
        before, after = [], []
        for f in range(field_count):
            tile = held[row, f, :, 0:LANES]
            for t in range(1, lon_count // LANES):
                tile = tile + held[row, f, :, t * LANES:(t + 1) * LANES]
            total = jnp.sum(tile, axis=0, keepdims=True)
            before.append(totals[f] + row_area * total)
            after.append(totals[field_count + f] + taken * total)
        return tuple(before + after)

    zero = jnp.zeros((1, LANES), jnp.float32)
    totals = lax.fori_loop(0, rows, add_row, (zero,) * (2 * field_count))
    part[0] = jnp.concatenate([*totals, jnp.zeros((8 - 2 * field_count, LANES), jnp.float32)], axis=0)

    def gather_small(copies, target, level):
        for copy in copies:
            copy.wait_recv()
        total = part[level]
        for k in range(len(copies)):
            total = total + target[k]
        return total

    for copy in ones:
        copy.start()
    for f in range(1, field_count):
        for dy in order:
            out_copy(f, dy).start()
    for dy in order:
        out_arrival(0, dy).wait_recv()
        start_halo(0, dy)
    for f in range(2, field_count):
        start_halo(f, 0)
    part[1] = gather_small(ones, met_one, 0)
    for copy in twos:
        copy.start()
    for dy in order:
        out_arrival(1, dy).wait_recv()
        start_halo(1, dy)
    part[2] = gather_small(twos, met_two, 1)
    for copy in threes:
        copy.start()
    for f in range(2, field_count):
        for dy in order:
            out_arrival(f, dy).wait_recv()
            start_halo(f, dy)
    for copy in to_smem:
        copy.wait()
    for copy in own_pieces:
        copy.wait()

    base = (group - 1) * span

    def interpolate(f, dy):
        to = ring_member(dy)

        def one_row(row, carry):
            place = whole_smem[to, 0, row] - base
            weight = [real_smem[to, a, row] for a in range(4)]
            for t in range(piece // LANES):
                at = pl.ds(t * LANES, LANES)
                total = weight[0] * window[f][place, :, at]
                for a in range(1, 4):
                    total = total + weight[a] * window[f][place + a, :, at]
                column[f][dy * rows + row, :, at] = total
            return carry

        lax.fori_loop(0, rows, one_row, 0)

    for f in range(field_count):
        for dy in (0, *order):
            for side in range(2):
                pl.when(has_side[1 - side])(lambda dy=dy, side=side: halo_arrival(f, dy, side).wait_recv())
        for dy in (2, 1, RING - 1, 0):
            interpolate(f, dy)
        for dy in (2, 1, RING - 1):
            back_copy(f, dy).start()
        back_own(f).start()

    sums_ref[...] = gather_small(threes, met_three, 2)

    for f in range(field_count):
        for dy in order:
            back_arrival(f, dy).wait_recv()
    for d in near:
        @pl.when(inside(d))
        def _(d=d):
            for copy in meta_copies(d):
                copy.wait_send()
    for copy in ones + twos + threes:
        copy.wait_send()
    for f in range(field_count):
        back_own(f).wait()
        for dy in order:
            out_copy(f, dy).wait_send()
            back_copy(f, dy).wait_send()
        for dy in (0, *order):
            for side in range(2):
                pl.when(has_side[side])(lambda f=f, dy=dy, side=side: halo_copy(f, dy, side).wait_send())


def exchange(lat_t, lon_t, departure_row, extents, area, fields):
    bands, levs = lax.axis_size("lat"), lax.axis_size("lev")
    rows, field_count, levels, lon_count = fields.shape
    crosses = bands // RING // DEEP
    piece = lon_count // RING
    tile = (8, LANES)
    dma = pltpu.SemaphoreType.DMA
    ones = RING * levs - 1
    near = 2 * REACH
    return pl.pallas_call(
        functools.partial(exchange_kernel, bands, levs),
        out_shape=(
            jax.ShapeDtypeStruct(fields.shape, fields.dtype),
            jax.ShapeDtypeStruct(tile, jnp.float32),
        ),
        in_specs=[pl.BlockSpec(memory_space=pltpu.SMEM)] * 5 + [pl.BlockSpec(memory_space=pl.ANY)],
        out_specs=(pl.BlockSpec(memory_space=pl.ANY), pl.BlockSpec(memory_space=pltpu.VMEM)),
        scratch_shapes=[
            pltpu.VMEM(fields.shape, jnp.float32),
            *[pltpu.VMEM((3 * RING * rows, levels, piece), jnp.float32) for _ in range(field_count)],
            *[pltpu.VMEM((RING * rows, levels, piece), jnp.float32) for _ in range(field_count)],
            pltpu.VMEM((near + 1,) + tile, jnp.float32),
            pltpu.VMEM((near + 1,) + tile, jnp.int32),
            pltpu.SMEM((RING,) + tile, jnp.float32),
            pltpu.SMEM((RING,) + tile, jnp.int32),
            pltpu.VMEM((3,) + tile, jnp.float32),
            pltpu.VMEM((ones,) + tile, jnp.float32),
            pltpu.VMEM((max(crosses - 1, 1),) + tile, jnp.float32),
            pltpu.VMEM((DEEP - 1,) + tile, jnp.float32),
            dma,
            dma((2, field_count)),
            dma((2,)),
            dma((2, near)),
            dma((2, near)),
            dma((field_count, RING - 1)),
            dma((field_count, RING - 1)),
            dma((2, field_count, RING)),
            dma((2, field_count, RING)),
            dma((field_count, RING - 1)),
            dma((field_count, RING - 1)),
            dma((ones,)),
            dma((ones,)),
            dma((max(crosses - 1, 1),)),
            dma((max(crosses - 1, 1),)),
            dma((DEEP - 1,)),
            dma((DEEP - 1,)),
        ],
        compiler_params=pltpu.CompilerParams(collective_id=0, has_side_effects=True),
        name="exchange",
    )(lat_t, lon_t, departure_row, extents, area, fields)


def row_kernel(lon_t_ref, shift_ref, sums_ref, column_ref, out_ref, doubled, ratio):
    row = pl.program_id(0)
    _, field_count, levels, lon_count = column_ref.shape
    tiles = lon_count // LANES

    @pl.when(row == 0)
    def _():
        for f in range(field_count):
            before = jnp.sum(sums_ref[f:f + 1, :], axis=1, keepdims=True)
            after = jnp.sum(sums_ref[field_count + f:field_count + f + 1, :], axis=1, keepdims=True)
            ratio[f] = jnp.broadcast_to(before / after, ratio.shape[1:])

    lon_w = cubic(lon_t_ref[row])
    lane = lax.broadcasted_iota(jnp.int32, (levels, LANES), 1)
    first = lax.rem(shift_ref[row] - 1 + lon_count, lon_count)
    whole, rest = first // LANES, lax.rem(first, LANES)
    turn = lax.rem(LANES - rest, LANES)
    keep = lane < LANES - rest

    def ahead(pieces, step):
        turned = [pltpu.roll(piece, LANES - step, 1) for piece in pieces]
        return [jnp.where(lane < LANES - step, turned[t], turned[(t + 1) % tiles]) for t in range(tiles)]

    for f in range(field_count):
        lon = [weight * ratio[f] for weight in lon_w]
        column = [column_ref[0, f, :, t * LANES:(t + 1) * LANES] for t in range(tiles)]
        after = ahead(column, 1)
        later = ahead([lon[2] * column[t] + lon[3] * after[t] for t in range(tiles)], 2)
        for t in range(tiles):
            mixed = lon[0] * column[t] + lon[1] * after[t] + later[t]
            doubled[f, :, t * LANES:(t + 1) * LANES] = mixed
            doubled[f, :, lon_count + t * LANES:lon_count + (t + 1) * LANES] = mixed
        turned = []
        for t in range(tiles + 1):
            at = pl.multiple_of((whole + t) * LANES, LANES)
            turned.append(pltpu.roll(doubled[f, :, pl.ds(at, LANES)], turn, 1))
        for t in range(tiles):
            out_ref[0, f, :, t * LANES:(t + 1) * LANES] = jnp.where(keep, turned[t], turned[t + 1])


def rows_of(lon_t, shift, sums, column):
    rows, field_count, levels, lon_count = column.shape
    smem = pl.BlockSpec(memory_space=pltpu.SMEM)
    block = pl.BlockSpec((1, field_count, levels, lon_count), lambda r: (r, 0, 0, 0))
    return pl.pallas_call(
        row_kernel,
        grid=(rows,),
        out_shape=jax.ShapeDtypeStruct(column.shape, column.dtype),
        in_specs=[smem, smem, pl.BlockSpec(memory_space=pltpu.VMEM), block],
        out_specs=block,
        scratch_shapes=[
            pltpu.VMEM((field_count, levels, 2 * lon_count), jnp.float32),
            pltpu.VMEM((field_count, levels, LANES), jnp.float32),
        ],
        compiler_params=pltpu.CompilerParams(dimension_semantics=("arbitrary",)),
        name="rows",
    )(lon_t, shift, sums, column)


def per_device(fields, lat_fraction, lon_fraction, lon_shift, departure_row, extents):
    bands = lax.axis_size("lat")
    total_rows = bands * fields.shape[0]
    row_ids = np.arange(total_rows)
    area = jnp.asarray(np.cos(math.pi * (row_ids + 0.5) / total_rows - math.pi / 2.0), jnp.float32)
    column, sums = exchange(lat_fraction, lon_fraction, departure_row, extents, area, fields)
    return rows_of(lon_fraction, lon_shift, sums, column)


def solution(mesh):
    return jax.shard_map(
        per_device,
        mesh=mesh,
        in_specs=(
            P("lat", None, "lev", None),
            P("lat"),
            P("lat"),
            P("lat"),
            P("lat"),
            P("lat", None),
        ),
        out_specs=P("lat", None, "lev", None),
        check_vma=False,
    )
```

time: 271 us -> 94.2 us (0.35)
  the two profiles are of different devices: /device:TPU:32 before, /device:TPU:1 now
where the time goes in v1:
time: 94.2 us; the launch traced here: 94 us
  Pallas kernels  94 us (100%)
    pallas_call x1, Pallas kernels, exchange(): pl.pallas_call(functools.partial(exchange_kernel, bands, levs), out_shape...  85.4 us
    pallas_call x1, Pallas kernels, rows_of(): pl.pallas_call(row_kernel, grid=(rows,), out_shape=jax.ShapeDtypeStruct(c...  8.52 us

profile of v1, /device:TPU:1, one launch (start us, length us, event | category | flops | bytes accessed | tf_op | source)
XLA Modules:
  0.0 94.0 jit_solution(7443413545915461901)
XLA Ops:
  0.0 85.4 %exchange.1 = (f32[10,3,8,2560]{3,2,1,0:T(8,128)}, f32[8,128]{1,0:T(8,128)}) custom-call(f32[10]{0:T(128)} %lat_t_ref.1, f32[10]{0:T(128)} %lon_t_ref.3, s32[10]{0:T(128)} %departure_ref.1, s32[1,2]{1,0:T(1,128)} %extents_ref.1, f32[1280]{0:T(1024)} %constant.2.clone.area_ref, f32[10,3,8,2560]{3,2,1,0:T(8,128)} %fields_ref.1), custom_call_target="tpu_custom_call" | custom-call | tf_op jit(solution)/shard_map/exchange/pallas_call | solution.py:369
  85.4 8.5 %rows.1 = f32[10,3,8,2560]{3,2,1,0:T(8,128)} custom-call(f32[10]{0:T(128)} %lon_t_ref.3, s32[10]{0:T(128)} %shift_ref.1, f32[8,128]{1,0:T(8,128)} %get-tuple-element.7.sums_ref, f32[10,3,8,2560]{3,2,1,0:T(8,128)} %get-tuple-element.8.column_ref), custom_call_target="tpu_custom_call" | custom-call | tf_op jit(solution)/shard_map/rows/pallas_call | solution.py:456
